TPU v7x, 256 devices: a 8x8x2 block of a 8x8x16 slice. The times are simulated.
256 devices in a mesh: vol: 2 (over z), row: 128 (over y, x, core).
Axes of the slice: x: 8, y: 8, z: 2, core: 2. Of those that a mesh axis runs over, the one named last changes fastest.
The devices are a block of a 8x8x16 slice.
Arguments:
- volume: float32 [6, 2048, 2048], P('vol', 'row'), parts along dimension 0, may hold values from 0.25 to 2
- psf_spectra: bfloat16 [2, 3, 2048, 2048], P(None, None, 'row'), may hold values from -3.5 to 3.5
- background: float32 [2048, 2048], P('row'), may hold values from 1 to 4
- measured: float32 [4096, 2048], P(('vol', 'row')), parts along dimension 0, may hold values from 0.5 to 4
Outputs:
- new_volume: float32 [6, 2048, 2048], P('vol', 'row'), parts along dimension 0
- projection: float32 [4096, 2048], P(('vol', 'row')), parts along dimension 0
There are 2 independent parts, one for each index of `vol`. A program takes and returns all parts, laid end to end along the dimension named above; an argument that names none is the same for every part. Nothing has to cross between parts.
All inputs are finite; a program needn't handle non-finite values.
Results may differ from a plain program's by a relative error of at most 0.0003.
Values sent between devices are 32-bit elements; how exact they have to be, the bound alone decides.
A program may use at most 64 MiB of HBM per device.

v0:
```python
import functools
import math

import jax
import jax.numpy as jnp
import ml_dtypes
import numpy as np
from jax import lax
from jax.experimental import pallas as pl
from jax.experimental.pallas import tpu as pltpu
from jax.sharding import PartitionSpec as P

FLOOR = 0.5
F32 = jnp.float32
BF16 = jnp.bfloat16
NN = (((1,), (0,)), ((), ()))
NT = (((1,), (1,)), ((), ()))


def split_np(table):
    hi = table.astype(np.float32).astype(ml_dtypes.bfloat16)
    lo = (table - hi.astype(np.float64)).astype(np.float32).astype(ml_dtypes.bfloat16)
    return np.stack([hi, lo])


def tables(n, q):
    length = n * q
    half = q // 2
    big = np.exp(-2j * np.pi * np.outer(np.arange(n), np.arange(n)) / n)
    small = np.exp(-2j * np.pi * np.outer(np.arange(q), np.arange(q)) / q)
    big_stack = np.block([[big.real, -big.imag], [big.imag, big.real]])
    spread = np.kron(small, np.eye(q))
    ycols = np.concatenate([spread.real, spread.imag], axis=0)
    mixed = np.einsum("xk,ij->ixkj", small, np.eye(half)).reshape(half * q, q * half)
    xmix = np.block([[mixed.real, mixed.imag], [-mixed.imag, mixed.real]])
    twist = np.exp(-2j * np.pi * np.outer(np.arange(q), np.arange(n)) / length)
    ytw = np.repeat(twist, q, axis=0)
    xtw = np.tile(twist.T, (1, half))
    pair = lambda z: np.stack([z.real, z.imag]).astype(np.float32)
    return (
        split_np(big_stack),
        split_np(ycols),
        split_np(np.ascontiguousarray(ycols.T)),
        split_np(xmix),
        pair(ytw),
        pair(ytw.T),
        pair(xtw),
    )


def split(value):
    hi = value.astype(BF16)
    return hi, (value - hi.astype(F32)).astype(BF16)


def dot3(left, right, dims):
    mul = functools.partial(lax.dot_general, dimension_numbers=dims, preferred_element_type=F32)
    return mul(left[0], right[0]) + mul(left[0], right[1]) + mul(left[1], right[0])


def kernel(
    n, q, slices,
    vol_ref, psf_ref, back_ref, meas_ref,
    big_ref, ycol_ref, yrow_ref, xmix_ref, ytw_ref, ytwt_ref, xtw_ref,
    out_ref, proj_ref,
    send_buf, recv_buf, resp, send_sems, recv_sems,
):
    half = q // 2
    lanes = half * q
    scale = 1.0 / (n * q * n * q)
    me = lax.axis_index("row")
    vol_id = lax.axis_index("vol")

    def peer(step):
        return lax.rem(me + step, n)

    barrier = pltpu.get_barrier_semaphore()

    @pl.loop(1, n)
    def _(step):
        pl.semaphore_signal(
            barrier, inc=1, device_id=(vol_id, peer(step)), device_id_type=pl.DeviceIdType.MESH
        )

    def table(ref):
        return ref[0], ref[1]

    def copy_to(slot, dst):
        return pltpu.make_async_remote_copy(
            src_ref=send_buf.at[slot, dst],
            dst_ref=recv_buf.at[slot, me],
            send_sem=send_sems.at[slot],
            recv_sem=recv_sems.at[slot],
            device_id=(vol_id, dst),
            device_id_type=pl.DeviceIdType.MESH,
        )

    def start(slot):
        @pl.loop(1, n)
        def _(step):
            copy_to(slot, peer(step)).start()

        recv_buf[slot, me] = send_buf[slot, me]

    def whole(slot):
        return pltpu.make_async_remote_copy(
            src_ref=send_buf.at[slot, pl.ds(0, n - 1)],
            dst_ref=recv_buf.at[slot, pl.ds(0, n - 1)],
            send_sem=send_sems.at[slot],
            recv_sem=recv_sems.at[slot],
            device_id=(vol_id, peer(1)),
            device_id_type=pl.DeviceIdType.MESH,
        )

    def put(slot, stacked, order):
        for place, part in enumerate(order):
            for h in range(2):
                send_buf[slot, :, part * 2 + h, :] = stacked[
                    place * n : (place + 1) * n, h * lanes : (h + 1) * lanes
                ]

    def get(slot, order):
        rows = []
        for part in order:
            rows.append(
                jnp.concatenate([recv_buf[slot, :, part * 2 + h, :] for h in range(2)], axis=1)
            )
        return jnp.concatenate(rows, axis=0)

    def stack_rows(read):
        return jnp.concatenate([read(a) for a in range(q)], axis=0)

    def y_forward(field, slot):
        mixed = dot3(table(ycol_ref), split(field), NN)
        re, im = mixed[: q * q], mixed[q * q :]
        wr, wi = ytw_ref[0], ytw_ref[1]
        turned = jnp.concatenate([re * wr - im * wi, re * wi + im * wr], axis=1)
        put(slot, dot3(table(big_ref), split(turned), NT), (0, 1))

    def x_forward(slot):
        got = dot3(table(big_ref), split(get(slot, (0, 1))), NN)
        wr, wi = xtw_ref[0], xtw_ref[1]
        rows = []
        for h in range(2):
            re = got[:n, h * lanes : (h + 1) * lanes]
            im = got[n:, h * lanes : (h + 1) * lanes]
            rows.append(jnp.concatenate([re * wr - im * wi, re * wi + im * wr], axis=1))
        spec = dot3(split(jnp.concatenate(rows, axis=0)), table(xmix_ref), NN)
        return spec[:, :lanes], spec[:, lanes:]

    def x_inverse(re, im, slot):
        mixed = dot3(split(jnp.concatenate([re, im], axis=1)), table(xmix_ref), NT)
        wr, wi = xtw_ref[0], xtw_ref[1]
        real_cols, imag_cols = [], []
        for h in range(2):
            re = mixed[h * n : (h + 1) * n, :lanes]
            im = mixed[h * n : (h + 1) * n, lanes:]
            real_cols.append(re * wr + im * wi)
            imag_cols.append(im * wr - re * wi)
        swapped = jnp.concatenate(
            [jnp.concatenate(imag_cols, axis=1), jnp.concatenate(real_cols, axis=1)], axis=0
        )
        put(slot, dot3(table(big_ref), split(swapped), NN), (1, 0))

    def y_inverse(slot):
        got = dot3(table(big_ref), split(get(slot, (1, 0))), NN)
        im, re = got[:n], got[n:]
        wr, wi = ytwt_ref[0], ytwt_ref[1]
        turned = jnp.concatenate([re * wr + im * wi, im * wr - re * wi], axis=1)
        return dot3(table(yrow_ref), split(turned), NT) * scale

    for d in range(slices):
        y_forward(stack_rows(lambda a: vol_ref[d, :, a * n : (a + 1) * n]), d)
        if d == 0:
            pl.semaphore_wait(barrier, n - 1)
        start(d)

    for part in range(2):
        for d in range(slices):
            for h in range(2):
                block = jnp.concatenate(
                    [
                        psf_ref[part, d, :, k * n : (k + 1) * n].astype(F32)[
                            h * half : (h + 1) * half
                        ]
                        for k in range(q)
                    ],
                    axis=0,
                )
                resp[part, d, h * n : (h + 1) * n, :] = block.T

    sum_re = sum_im = None
    for d in range(slices):
        whole(d).wait_recv()
        re, im = x_forward(d)
        rr, ri = resp[0, d], resp[1, d]
        pr, pi = re * rr - im * ri, re * ri + im * rr
        sum_re = pr if d == 0 else sum_re + pr
        sum_im = pi if d == 0 else sum_im + pi
    x_inverse(sum_re, sum_im, slices)
    start(slices)
    whole(slices).wait_recv()
    projection = y_inverse(slices)
    quotient = []
    for a in range(q):
        cols = slice(a * n, (a + 1) * n)
        piece = projection[a * q : (a + 1) * q]
        proj_ref[:, cols] = piece
        quotient.append(meas_ref[:, cols] / jnp.maximum(piece + back_ref[:, cols], FLOOR))
    y_forward(jnp.concatenate(quotient, axis=0), slices + 1)
    start(slices + 1)
    whole(slices + 1).wait_recv()
    qr, qi = x_forward(slices + 1)
    for d in range(slices):
        rr, ri = resp[0, d], resp[1, d]
        x_inverse(qr * rr + qi * ri, qi * rr - qr * ri, slices + 2 + d)
        start(slices + 2 + d)
    for d in range(slices):
        whole(slices + 2 + d).wait_recv()
        correction = y_inverse(slices + 2 + d)
        for a in range(q):
            cols = slice(a * n, (a + 1) * n)
            out_ref[d, :, cols] = vol_ref[d, :, cols] * correction[a * q : (a + 1) * q]
    for slot in range(2 * slices + 2):
        whole(slot).wait_send()


def shards(volume, psf_spectra, background, measured):
    n = lax.axis_size("row")
    slices, q, length = volume.shape
    slots = 2 * slices + 2
    consts = tables(n, q)
    in_vmem = pl.BlockSpec(memory_space=pltpu.VMEM)
    return pl.pallas_call(
        functools.partial(kernel, n, q, slices),
        out_shape=(
            jax.ShapeDtypeStruct(volume.shape, F32),
            jax.ShapeDtypeStruct(measured.shape, F32),
        ),
        in_specs=[in_vmem] * (4 + len(consts)),
        out_specs=(in_vmem, in_vmem),
        scratch_shapes=[
            pltpu.VMEM((slots, n, 4, q * q // 2), F32),
            pltpu.VMEM((slots, n, 4, q * q // 2), F32),
            pltpu.VMEM((2, slices, 2 * n, q * q // 2), F32),
            pltpu.SemaphoreType.DMA((slots,)),
            pltpu.SemaphoreType.DMA((slots,)),
        ],
        compiler_params=pltpu.CompilerParams(
            collective_id=0, has_side_effects=True, vmem_limit_bytes=60 * 1024 * 1024
        ),
    )(volume, psf_spectra, background, measured, *consts)


def solution(mesh):
    in_specs = (
        P("vol", "row", None),
        P(None, None, "row", None),
        P("row", None),
        P(("vol", "row"), None),
    )
    out_specs = (P("vol", "row", None), P(("vol", "row"), None))
    return jax.shard_map(shards, mesh=mesh, in_specs=in_specs, out_specs=out_specs, check_vma=False)
```

profile of v0, /device:TPU:513, one launch (start us, length us, event | category | flops | bytes accessed | tf_op | source)
XLA Modules:
  0.0 102.4 jit_solution(1533856321404680927)
XLA Ops:
  0.6 99.3 %shard_map.122 = (f32[3,16,2048]{2,1,0:T(8,128)}, f32[16,2048]{1,0:T(8,128)}) custom-call(f32[3,16,2048]{2,1,0:T(8,128)} %vol_ref.1, bf16[2,3,16,2048]{3,2,1,0:T(8,128)(2,1)} %psf_ref.1, f32[16,2048]{1,0:T(8,128)} %back_ref.1, f32[16,2048]{1,0:T(8,128)} %meas_ref.1, bf16[2,256,256]{2,1,0:T(8,128)(2,1)} %constant.14.clone.big_ref, ...), custom_call_target="tpu_custom_call" | custom-call | tf_op jit(solution)/shard_map/pallas_call | solution.py:234
  99.9 0.0 copy-start
  100.0 1.8 %copy.15 = f32[3,16,2048]{2,1,0:T(8,128)} copy(f32[3,16,2048]{2,1,0:T(8,128)} %get-tuple-element.4) | data formatting | bytes 786432
  101.8 0.0 copy-done
  101.8 0.7 copy.16
Async XLA Ops:
  99.9 1.8 %copy-start = (f32[16,2048]{1,0:T(8,128)S(1)}, f32[16,2048]{1,0:T(8,128)}, u32[]{:S(2)}) copy-start(f32[16,2048]{1,0:T(8,128)} %get-tuple-element.5) | copy-start | bytes 393220
where the time goes:
time: 103 us; the launch traced here: 102 us
  Pallas kernels  99.3 us (96%)
  local copies, waits for them, and re-layouts  2.46 us (2%)
    pallas_call x1, Pallas kernels, shards(): pl.pallas_call(functools.partial(kernel, n, q, slices), out_shape=(jax.Sh...  99.3 us
    unnamed x4, local copies, waits for them, and re-layouts  2.46 us

commit v1 on v0

v1 whole, which is shorter than its diff:
```python
import functools

import jax
import jax.numpy as jnp
import ml_dtypes
import numpy as np
from jax import lax
from jax.experimental import pallas as pl
from jax.experimental.pallas import tpu as pltpu
from jax.sharding import PartitionSpec as P

FLOOR = 0.5
F32 = jnp.float32
BF16 = jnp.bfloat16
NN = (((1,), (0,)), ((), ()))
NT = (((1,), (1,)), ((), ()))
GROUPS = ((0, 1), (2,))


def split_np(table):
    hi = table.astype(np.float32).astype(ml_dtypes.bfloat16)
    lo = (table - hi.astype(np.float64)).astype(np.float32).astype(ml_dtypes.bfloat16)
    return np.stack([hi, lo])


def tables(n, q):
    length = n * q
    half = q // 2
    lanes = half * q
    big = np.exp(-2j * np.pi * np.outer(np.arange(n), np.arange(n)) / n)
    small = np.exp(-2j * np.pi * np.outer(np.arange(q), np.arange(q)) / q)
    big_stack = np.block([[big.real, -big.imag], [big.imag, big.real]])
    spread = np.kron(small[: half + 1], np.eye(q))
    ycols = np.concatenate([spread.real, spread.imag], axis=0)
    yrows = np.zeros((q * q, 2, 2 * lanes))
    yrows[:, 0, : (half + 1) * q] = spread.real.T
    yrows[:, 1, : (half + 1) * q] = spread.imag.T
    mixed = np.einsum("xk,ij->ixkj", small, np.eye(half)).reshape(lanes, q * half)
    xmix = np.block([[mixed.real, mixed.imag], [-mixed.imag, mixed.real]])
    twist = np.exp(-2j * np.pi * np.outer(np.arange(q), np.arange(n)) / length)
    ytw = np.repeat(twist[: half + 1], q, axis=0)
    ytwt = np.zeros((n, 2 * lanes), complex)
    ytwt[:, : (half + 1) * q] = ytw.T
    xtw = np.tile(twist.T, (1, half))
    pair = lambda z: np.stack([z.real, z.imag]).astype(np.float32)
    return (
        split_np(ycols),
        pair(ytw),
        split_np(big_stack),
        pair(xtw),
        split_np(xmix),
        pair(ytwt),
        split_np(yrows.reshape(q * q, 4 * lanes)),
    )


def split(value):
    hi = value.astype(BF16)
    return hi, (value - hi.astype(F32)).astype(BF16)


def dot(left, right, dims):
    return lax.dot_general(left, right, dimension_numbers=dims, preferred_element_type=F32)


def dot3(left, right, dims):
    return dot(left[0], right[0], dims) + dot(left[0], right[1], dims) + dot(left[1], right[0], dims)


def kernel(n, q, slices, counts, *refs):
    ins, refs = refs[:11], refs[11:]
    out_ref, proj_ref = refs[:2]
    held, refs = refs[2:13], refs[13:]
    messages = len(counts)
    sends, recvs = refs[:messages], refs[messages : 2 * messages]
    (
        own_half, main_send, main_recv, row_send, row_self, row_recv, resp, resp_mix, spec, spec_mix, total,
        in_sems, send_sems, recv_sems, psf_sems, row_sems, late_sem,
    ) = refs[2 * messages :]
    vol_ref, psf_ref, back_ref, meas_ref, ycol_ref, ytw_ref, big_ref, xtw_ref, xmix_ref, ytwt_ref, yrow_ref = held
    order = (1, 0, 4, 5, 6, 7, 8, 9, 10, 2, 3)
    parts = len(GROUPS)
    half = q // 2
    middle = n // 2
    scale = 1.0 / (n * q * n * q)
    me = lax.axis_index("row")
    vol_id = lax.axis_index("vol")
    row_iota = lax.broadcasted_iota(jnp.int32, (n, n), 0)
    lane_iota = lax.broadcasted_iota(jnp.int32, (n, n), 1)

    def fetch(i):
        return pltpu.make_async_copy(ins[i], held[i], in_sems.at[i])

    for i in order:
        fetch(i).start()

    def device(dst):
        return (vol_id, dst)

    def tell(sem, dst):
        pl.semaphore_signal(sem, inc=1, device_id=device(dst), device_id_type=pl.DeviceIdType.MESH)

    barrier = pltpu.get_barrier_semaphore()

    def peer(step):
        return jnp.bitwise_and(me + step, n - 1)

    @pl.when(me < 2)
    def _():
        tell(barrier, 1 - me)

    @pl.when(me >= 2)
    def _():
        @pl.loop(1, n)
        def _(step):
            tell(barrier, peer(step))

    def copy_to(m, dst):
        return pltpu.make_async_remote_copy(
            src_ref=sends[m].at[dst],
            dst_ref=recvs[m].at[me],
            send_sem=send_sems.at[m],
            recv_sem=recv_sems.at[m],
            device_id=device(dst),
            device_id_type=pl.DeviceIdType.MESH,
        )

    def start(m):
        @pl.loop(1, n, unroll=8)
        def _(step):
            copy_to(m, peer(step)).start()

        recvs[m][me] = sends[m][me]

    def whole(m):
        return pltpu.make_async_remote_copy(
            src_ref=sends[m].at[pl.ds(0, n - 1)],
            dst_ref=recvs[m].at[pl.ds(0, n - 1)],
            send_sem=send_sems.at[m],
            recv_sem=recv_sems.at[m],
            device_id=device(peer(1)),
            device_id_type=pl.DeviceIdType.MESH,
        )

    def main_copy(dst):
        return pltpu.make_async_remote_copy(
            src_ref=main_send,
            dst_ref=main_recv,
            send_sem=psf_sems.at[0],
            recv_sem=psf_sems.at[1],
            device_id=device(dst),
            device_id_type=pl.DeviceIdType.MESH,
        )

    def row_copy(dst):
        return pltpu.make_async_remote_copy(
            src_ref=row_send,
            dst_ref=row_recv,
            send_sem=row_sems.at[0],
            recv_sem=row_sems.at[1],
            device_id=device(dst),
            device_id_type=pl.DeviceIdType.MESH,
        )

    def table(ref):
        return ref[0], ref[1]

    def y_forward(field, m, at):
        mixed = dot3(table(ycol_ref), split(field), NN)
        kept = (half + 1) * q
        re, im = mixed[:kept], mixed[kept:]
        wr, wi = ytw_ref[0], ytw_ref[1]
        turned = jnp.concatenate([re * wr - im * wi, re * wi + im * wr], axis=1)
        both = jnp.concatenate([turned[: half * q], turned[half * q :], turned[q : half * q]], axis=0)
        got = dot3(table(big_ref), split(both), NT)
        lanes = half * q
        re = jnp.concatenate([got[:middle, lanes:], got[middle:n, :lanes]], axis=0)
        im = jnp.concatenate([got[n : n + middle, lanes:], got[n + middle :, :lanes]], axis=0)
        im = jnp.where((row_iota == middle) & (lane_iota < q), got[0:1, :lanes], im)
        sends[m][:, 2 * at, :] = re
        sends[m][:, 2 * at + 1, :] = im

    def x_forward(re, im):
        got = dot3(table(big_ref), split(jnp.concatenate([re, im], axis=0)), NN)
        re, im = got[:n], got[n:]
        wr, wi = xtw_ref[0], xtw_ref[1]
        turned = jnp.concatenate([re * wr - im * wi, re * wi + im * wr], axis=1)
        out = dot3(split(turned), table(xmix_ref), NN)
        return out[:, :n], out[:, n:]

    def x_forward_conj(fields):
        re_sum = im_sum = jnp.zeros((n, n), F32)
        for d, (re, im) in enumerate(fields):
            mine = (lane_iota >= d * q) & (lane_iota < (d + 1) * q)
            if d:
                re, im = pltpu.roll(re, d * q, 1), pltpu.roll(im, d * q, 1)
            re_sum = jnp.where(mine, re, re_sum)
            im_sum = jnp.where(mine, -im, im_sum)
        return x_forward(re_sum, im_sum)

    def x_inverse(re, im, m, at):
        mixed = dot3(split(jnp.concatenate([re, im], axis=1)), table(xmix_ref), NT)
        wr, wi = xtw_ref[0], xtw_ref[1]
        re, im = mixed[:, :n], mixed[:, n:]
        swapped = jnp.concatenate([im * wr - re * wi, re * wr + im * wi], axis=0)
        got = dot3(table(big_ref), split(swapped), NN)
        sends[m][:, 2 * at, :] = got[n:]
        sends[m][:, 2 * at + 1, :] = got[:n]

    def y_inverse(m, at):
        re, im = recvs[m][:, 2 * at, :], recvs[m][:, 2 * at + 1, :]
        first = lane_iota < q
        upper = first & (row_iota < middle)
        zero_row = first & (row_iota == 0)
        mid_row = first & (row_iota == middle)
        re_low = jnp.where(upper, 0.0, re)
        re_low = jnp.where(mid_row, 0.5 * re, re_low)
        re_low = jnp.where(zero_row, 0.5 * im[middle : middle + 1], re_low)
        im_low = jnp.where(upper | mid_row, 0.0, im)
        re_high, im_high = jnp.where(upper, re, 0.0), jnp.where(upper, im, 0.0)
        swapped = jnp.concatenate(
            [
                jnp.concatenate([im_low, im_high], axis=1),
                jnp.concatenate([re_low, re_high], axis=1),
            ],
            axis=0,
        )
        got = dot3(table(big_ref), split(swapped), NN)
        im, re = got[:n], got[n:]
        wr, wi = ytwt_ref[0], ytwt_ref[1]
        turned = jnp.concatenate([re * wr + im * wi, im * wr - re * wi], axis=1)
        return dot3(table(yrow_ref), split(turned), NT) * (2.0 * scale)

    fetch(1).wait()
    reverse = jnp.where((row_iota + lane_iota == n) | (row_iota + lane_iota == 0), 1.0, 0.0).astype(BF16)
    same_block = row_iota // half == lane_iota // half
    slot_sum = row_iota % half + lane_iota % half
    slot_flip = jnp.where(same_block & ((slot_sum == half) | (slot_sum == 0)), 1.0, 0.0).astype(BF16)

    def blocks(field, backwards):
        places = range(q - 1, -1, -1) if backwards else range(q)
        return jnp.concatenate([field[:, k * n : (k + 1) * n] for k in places], axis=0)

    def mend(field):
        return jnp.where(row_iota == 0, pltpu.roll(field, half, 1), field)

    sub_iota = lax.broadcasted_iota(jnp.int32, (half, n * q), 0)
    rows = []
    for part in range(2):
        for d in range(slices):
            at = part * slices + d
            sign = 0.5 if part == 0 else -0.5
            both = psf_ref[part, d].astype(F32)
            low, high = both[:half], both[half:]
            rows.append(low[0:1])
            own = jnp.where((sub_iota == 0) & (me < middle), high, low)
            own_half[at] = 0.5 * blocks(own, False).T
            turned = dot(reverse, blocks(high, True).astype(BF16), NT)
            turned = dot(turned.astype(BF16), slot_flip, NN)
            main_send[at] = sign * mend(turned)
    packed = jnp.concatenate(rows + [jnp.zeros((half - 2 * slices, n * q), F32)], axis=0)
    turned = mend(dot(reverse, blocks(packed, True).astype(BF16), NT))
    mine = jnp.where(lane_iota % half < slices, 0.5, -0.5) * turned
    row_self[...] = mine
    row_send[...] = jnp.where(me == 0, mine + 0.5 * blocks(packed, False).T, mine)

    @pl.when(me >= 2)
    def _():
        pl.semaphore_wait(barrier, n - 3)

    @pl.when(me < 2)
    def _():
        pl.semaphore_wait(barrier, n - 1)

        @pl.when(me == 1)
        def _():
            @pl.loop(2, n)
            def _(dst):
                tell(late_sem, dst)

    @pl.when(me < n - 2)
    def _():
        main_copy(n - 1 - me).start()

    @pl.when(me == 0)
    def _():
        row_copy(middle).start()

    @pl.when((me > 0) & (me < middle))
    def _():
        row_copy(n - me).start()

    for i in (0, 4, 5, 6):
        fetch(i).wait()
    for m, group in enumerate(GROUPS):
        for at, d in enumerate(group):
            y_forward(
                jnp.concatenate([vol_ref[d, :, a * n : (a + 1) * n] for a in range(q)], axis=0), m, at
            )

        @pl.when(me >= 2)
        def _():
            @pl.loop(1, n - 2, unroll=5)
            def _(step):
                place = me + step
                copy_to(m, jnp.where(place >= n, place - (n - 2), place)).start()

        @pl.when(me < 2)
        def _():
            @pl.loop(1, n, unroll=8)
            def _(step):
                copy_to(m, peer(step)).start()

        recvs[m][me] = sends[m][me]

    @pl.when(me >= 2)
    def _():
        pl.semaphore_wait(late_sem, 1)
        for dst in range(2):
            for m in range(parts):
                copy_to(m, dst).start()

    @pl.when(me >= n - 2)
    def _():
        main_copy(n - 1 - me).start()

    main_copy(n - 1 - me).wait_recv()
    slot_zero = lane_iota % half == 0
    for at in range(2 * slices):
        resp[at] = own_half[at] + main_recv[at]

    def spread(field, at):
        return pltpu.roll(field, n - at, 1) if at else field

    @pl.when(me >= middle)
    def _():
        row_copy(middle).wait_recv()
        other = jnp.where(me == middle, row_self[...], row_recv[...])
        for at in range(2 * slices):
            resp[at] = jnp.where(slot_zero, own_half[at] + spread(other, at), resp[at])

    @pl.when(me == middle)
    def _():
        for at in range(2 * slices):
            edge = spread(row_recv[...], at)
            here = resp[at]
            resp[at] = jnp.where(slot_zero, 0.5 * (here + edge), here)
            resp_mix[at] = jnp.where(slot_zero, 0.5 * (here - edge), 0.0)

    for i in (7, 8):
        fetch(i).wait()
    for m, group in enumerate(GROUPS):
        whole(m).wait_recv()
        for at, d in enumerate(group):
            re, im = x_forward(recvs[m][:, 2 * at, :], recvs[m][:, 2 * at + 1, :])
            spec[0, d] = re
            spec[1, d] = im

    @pl.when(me == middle)
    def _():
        re, im = x_forward_conj(
            [
                (recvs[m][:, 2 * at, :], recvs[m][:, 2 * at + 1, :])
                for m, group in enumerate(GROUPS)
                for at, _ in enumerate(group)
            ]
        )
        spec_mix[0] = re
        spec_mix[1] = im

    sum_re = sum_im = jnp.zeros((n, n), F32)
    for d in range(slices):
        re, im = spec[0, d], spec[1, d]
        rr, ri = resp[d], resp[slices + d]
        sum_re = sum_re + (re * rr - im * ri)
        sum_im = sum_im + (re * ri + im * rr)
    total[0] = sum_re
    total[1] = sum_im

    @pl.when(me == middle)
    def _():
        sum_re, sum_im = total[0], total[1]
        for d in range(slices):
            re, im = spread(spec_mix[0], d), spread(spec_mix[1], d)
            rr, ri = resp_mix[d], resp_mix[slices + d]
            sum_re = sum_re + (re * rr - im * ri)
            sum_im = sum_im + (re * ri + im * rr)
        total[0] = sum_re
        total[1] = sum_im

    x_inverse(total[0], total[1], parts, 0)
    start(parts)
    for i in (9, 10, 2, 3):
        fetch(i).wait()
    whole(parts).wait_recv()
    projection = y_inverse(parts, 0)
    quotient = []
    for a in range(q):
        cols = slice(a * n, (a + 1) * n)
        piece = projection[a * q : (a + 1) * q]
        proj_ref[:, cols] = piece
        quotient.append(meas_ref[:, cols] / jnp.maximum(piece + back_ref[:, cols], FLOOR))

    y_forward(jnp.concatenate(quotient, axis=0), parts + 1, 0)
    start(parts + 1)
    whole(parts + 1).wait_recv()
    re, im = x_forward(recvs[parts + 1][:, 0, :], recvs[parts + 1][:, 1, :])
    spec[0, 0] = re
    spec[1, 0] = im

    @pl.when(me == middle)
    def _():
        re, im = x_forward_conj([(recvs[parts + 1][:, 0, :], recvs[parts + 1][:, 1, :])])
        spec_mix[0] = re
        spec_mix[1] = im

    for m, group in enumerate(GROUPS, start=parts + 2):
        for at, d in enumerate(group):
            re, im = spec[0, 0], spec[1, 0]
            rr, ri = resp[d], resp[slices + d]
            total[0] = re * rr + im * ri
            total[1] = im * rr - re * ri

            @pl.when(me == middle)
            def _():
                re, im = spec_mix[0], spec_mix[1]
                rr, ri = resp_mix[d], resp_mix[slices + d]
                total[0] = total[0] + (re * rr + im * ri)
                total[1] = total[1] + (im * rr - re * ri)

            x_inverse(total[0], total[1], m, at)
        start(m)
    for m, group in enumerate(GROUPS, start=parts + 2):
        whole(m).wait_recv()
        for at, d in enumerate(group):
            correction = y_inverse(m, at)
            for a in range(q):
                cols = slice(a * n, (a + 1) * n)
                out_ref[d, :, cols] = vol_ref[d, :, cols] * correction[a * q : (a + 1) * q]
    for m in range(messages):
        whole(m).wait_send()
    main_copy(n - 1 - me).wait_send()

    @pl.when(me < middle)
    def _():
        row_copy(middle).wait_send()


def shards(volume, psf_spectra, background, measured):
    n = lax.axis_size("row")
    slices, q, length = volume.shape
    consts = tables(n, q)
    args = (volume, psf_spectra, background, measured, *consts)
    grouped = [2 * len(group) for group in GROUPS]
    counts = grouped + [2, 2] + grouped
    in_vmem = pl.BlockSpec(memory_space=pltpu.VMEM)
    in_hbm = pl.BlockSpec(memory_space=pltpu.HBM)
    exchanged = [pltpu.VMEM((n, count, n), F32) for count in counts]
    tile = lambda *lead: pltpu.VMEM((*lead, n, n), F32)
    return pl.pallas_call(
        functools.partial(kernel, n, q, slices, counts),
        out_shape=(
            jax.ShapeDtypeStruct(volume.shape, F32),
            jax.ShapeDtypeStruct(measured.shape, F32),
        ),
        in_specs=[in_hbm] * len(args),
        out_specs=(in_vmem, in_vmem),
        scratch_shapes=[pltpu.VMEM(arg.shape, arg.dtype) for arg in args]
        + exchanged
        + exchanged
        + [
            tile(2 * slices),
            tile(2 * slices),
            tile(2 * slices),
            tile(),
            tile(),
            tile(),
            tile(2 * slices),
            tile(2 * slices),
            tile(2, slices),
            tile(2),
            tile(2),
            pltpu.SemaphoreType.DMA((len(args),)),
            pltpu.SemaphoreType.DMA((len(counts),)),
            pltpu.SemaphoreType.DMA((len(counts),)),
            pltpu.SemaphoreType.DMA((2,)),
            pltpu.SemaphoreType.DMA((2,)),
            pltpu.SemaphoreType.REGULAR,
        ],
        compiler_params=pltpu.CompilerParams(
            collective_id=0, has_side_effects=True, vmem_limit_bytes=60 * 1024 * 1024
        ),
    )(*args)


def solution(mesh):
    in_specs = (
        P("vol", "row", None),
        P(None, None, "row", None),
        P("row", None),
        P(("vol", "row"), None),
    )
    out_specs = (P("vol", "row", None), P(("vol", "row"), None))
    return jax.shard_map(shards, mesh=mesh, in_specs=in_specs, out_specs=out_specs, check_vma=False)
```

time: 103 us -> 95.8 us (0.930)
  Pallas kernels: 99.3 us -> 92.6 us
    pallas_call x1, Pallas kernels: 99.3 us -> 92.6 us  [shards(): pl.pallas_call(functools.partial(kernel, n, q, slices, counts), out_shape...]
where the time goes in v1:
time: 95.8 us; the launch traced here: 95.7 us
  Pallas kernels  92.6 us (97%)
  local copies, waits for them, and re-layouts  2.46 us (3%)
    pallas_call x1, Pallas kernels, shards(): pl.pallas_call(functools.partial(kernel, n, q, slices, counts), out_shape...  92.6 us
    unnamed x4, local copies, waits for them, and re-layouts  2.46 us

profile of v1, /device:TPU:513, one launch (start us, length us, event | category | flops | bytes accessed | tf_op | source)
XLA Modules:
  0.0 95.7 jit_solution(690230785455980565)
XLA Ops:
  0.6 92.6 %shard_map.122 = (f32[3,16,2048]{2,1,0:T(8,128)}, f32[16,2048]{1,0:T(8,128)}) custom-call(f32[3,16,2048]{2,1,0:T(8,128)} %refs_0_.1, bf16[2,3,16,2048]{3,2,1,0:T(8,128)(2,1)} %refs_1_.1, f32[16,2048]{1,0:T(8,128)} %refs_2_.1, f32[16,2048]{1,0:T(8,128)} %refs_3_.1, bf16[2,288,256]{2,1,0:T(8,128)(2,1)} %constant.14.clone.refs_4_, ...), custom_call_target="tpu_custom_call" | custom-call | tf_op jit(solution)/shard_map/pallas_call | solution.py:460
  93.2 0.0 copy-start
  93.2 1.8 %copy.15 = f32[3,16,2048]{2,1,0:T(8,128)} copy(f32[3,16,2048]{2,1,0:T(8,128)} %get-tuple-element.4) | data formatting | bytes 786432
  95.0 0.0 copy-done
  95.0 0.7 copy.16
Async XLA Ops:
  93.2 1.8 %copy-start = (f32[16,2048]{1,0:T(8,128)S(1)}, f32[16,2048]{1,0:T(8,128)}, u32[]{:S(2)}) copy-start(f32[16,2048]{1,0:T(8,128)} %get-tuple-element.5) | copy-start | bytes 393220

commit v2 on v1

--- a/solution.py
+++ b/solution.py
@@ -14,7 +14,8 @@
 BF16 = jnp.bfloat16
 NN = (((1,), (0,)), ((), ()))
 NT = (((1,), (1,)), ((), ()))
-GROUPS = ((0, 1), (2,))
+HEAD_GROUPS = ((0, 1, 2),)
+TAIL_GROUPS = ((0, 1), (2,))
 
 
 def split_np(table):
@@ -67,7 +68,7 @@
     return dot(left[0], right[0], dims) + dot(left[0], right[1], dims) + dot(left[1], right[0], dims)
 
 
-def kernel(n, q, slices, counts, *refs):
+def kernel(n, q, slices, counts, shares, *refs):
     ins, refs = refs[:11], refs[11:]
     out_ref, proj_ref = refs[:2]
     held, refs = refs[2:13], refs[13:]
@@ -75,16 +76,24 @@
     sends, recvs = refs[:messages], refs[messages : 2 * messages]
     (
         own_half, main_send, main_recv, row_send, row_self, row_recv, resp, resp_mix, spec, spec_mix, total,
-        in_sems, send_sems, recv_sems, psf_sems, row_sems, late_sem,
+        in_sems, send_sems, recv_sems, psf_sems, pass_sems, row_sems, late_sem, both_sem, pass_sem,
     ) = refs[2 * messages :]
     vol_ref, psf_ref, back_ref, meas_ref, ycol_ref, ytw_ref, big_ref, xtw_ref, xmix_ref, ytwt_ref, yrow_ref = held
     order = (1, 0, 4, 5, 6, 7, 8, 9, 10, 2, 3)
-    parts = len(GROUPS)
+    parts = len(HEAD_GROUPS)
     half = q // 2
     middle = n // 2
     scale = 1.0 / (n * q * n * q)
     me = lax.axis_index("row")
     vol_id = lax.axis_index("vol")
+    share = lax.rem(vol_id, shares)
+    other_vol = vol_id + (1 - 2 * share)
+    tiles = range(2 * slices)
+
+    def owned(at, mine=True):
+        owner = 0 if shares == 1 or at < 2 * slices * 2 // 3 else 1
+        return (share == owner) if mine else (share != owner)
+
     row_iota = lax.broadcasted_iota(jnp.int32, (n, n), 0)
     lane_iota = lax.broadcasted_iota(jnp.int32, (n, n), 1)
 
@@ -94,11 +103,11 @@
     for i in order:
         fetch(i).start()
 
-    def device(dst):
-        return (vol_id, dst)
-
-    def tell(sem, dst):
-        pl.semaphore_signal(sem, inc=1, device_id=device(dst), device_id_type=pl.DeviceIdType.MESH)
+    def device(dst, vol=None):
+        return (vol_id if vol is None else vol, dst)
+
+    def tell(sem, dst, vol=None):
+        pl.semaphore_signal(sem, inc=1, device_id=device(dst, vol), device_id_type=pl.DeviceIdType.MESH)
 
     barrier = pltpu.get_barrier_semaphore()
 
@@ -108,6 +117,12 @@
     @pl.when(me < 2)
     def _():
         tell(barrier, 1 - me)
+
+    if shares == 2:
+
+        @pl.when(me == 2)
+        def _():
+            tell(barrier, me, other_vol)
 
     @pl.when(me >= 2)
     def _():
@@ -142,15 +157,29 @@
             device_id_type=pl.DeviceIdType.MESH,
         )
 
-    def main_copy(dst):
+    def main_copy(at):
         return pltpu.make_async_remote_copy(
-            src_ref=main_send,
-            dst_ref=main_recv,
-            send_sem=psf_sems.at[0],
-            recv_sem=psf_sems.at[1],
-            device_id=device(dst),
+            src_ref=main_send.at[at],
+            dst_ref=main_recv.at[at],
+            send_sem=psf_sems.at[0, at],
+            recv_sem=psf_sems.at[1, at],
+            device_id=device(n - 1 - me),
             device_id_type=pl.DeviceIdType.MESH,
         )
+
+    def pass_copy(at):
+        return pltpu.make_async_remote_copy(
+            src_ref=main_recv.at[at],
+            dst_ref=main_recv.at[at],
+            send_sem=pass_sems.at[0, at],
+            recv_sem=pass_sems.at[1, at],
+            device_id=device(me, other_vol),
+            device_id_type=pl.DeviceIdType.MESH,
+        )
+
+    def each_tile(act, mine=True):
+        for at in tiles:
+            pl.when(owned(at, mine))(functools.partial(act, at))
 
     def row_copy(dst):
         return pltpu.make_async_remote_copy(
@@ -249,22 +278,30 @@
     for part in range(2):
         for d in range(slices):
             at = part * slices + d
-            sign = 0.5 if part == 0 else -0.5
             both = psf_ref[part, d].astype(F32)
             low, high = both[:half], both[half:]
             rows.append(low[0:1])
             own = jnp.where((sub_iota == 0) & (me < middle), high, low)
             own_half[at] = 0.5 * blocks(own, False).T
-            turned = dot(reverse, blocks(high, True).astype(BF16), NT)
-            turned = dot(turned.astype(BF16), slot_flip, NN)
-            main_send[at] = sign * mend(turned)
+
+    def prepare(at):
+        high = psf_ref[at // slices, at % slices].astype(F32)[half:]
+        turned = dot(reverse, blocks(high, True).astype(BF16), NT)
+        turned = dot(turned.astype(BF16), slot_flip, NN)
+        main_send[at] = (0.5 if at < slices else -0.5) * mend(turned)
+
+    each_tile(prepare)
     packed = jnp.concatenate(rows + [jnp.zeros((half - 2 * slices, n * q), F32)], axis=0)
     turned = mend(dot(reverse, blocks(packed, True).astype(BF16), NT))
     mine = jnp.where(lane_iota % half < slices, 0.5, -0.5) * turned
     row_self[...] = mine
     row_send[...] = jnp.where(me == 0, mine + 0.5 * blocks(packed, False).T, mine)
 
-    @pl.when(me >= 2)
+    @pl.when(me == 2)
+    def _():
+        pl.semaphore_wait(barrier, n - 4 + shares)
+
+    @pl.when(me > 2)
     def _():
         pl.semaphore_wait(barrier, n - 3)
 
@@ -272,15 +309,17 @@
     def _():
         pl.semaphore_wait(barrier, n - 1)
 
-        @pl.when(me == 1)
-        def _():
-            @pl.loop(2, n)
-            def _(dst):
-                tell(late_sem, dst)
-
-    @pl.when(me < n - 2)
-    def _():
-        main_copy(n - 1 - me).start()
+    @pl.when(me == 1)
+    def _():
+        @pl.loop(2, n)
+        def _(dst):
+            tell(late_sem, dst)
+
+    @pl.when(me >= n - 2)
+    def _():
+        pl.semaphore_wait(late_sem, 1)
+
+    each_tile(lambda at: main_copy(at).start())
 
     @pl.when(me == 0)
     def _():
@@ -292,11 +331,13 @@
 
     for i in (0, 4, 5, 6):
         fetch(i).wait()
-    for m, group in enumerate(GROUPS):
+    for m, group in enumerate(HEAD_GROUPS):
         for at, d in enumerate(group):
             y_forward(
                 jnp.concatenate([vol_ref[d, :, a * n : (a + 1) * n] for a in range(q)], axis=0), m, at
             )
+
+    for m in range(parts):
 
         @pl.when(me >= 2)
         def _():
@@ -313,18 +354,52 @@
 
         recvs[m][me] = sends[m][me]
 
+    @pl.when((me >= 2) & (me < n - 2))
+    def _():
+        pl.semaphore_wait(late_sem, 1)
+
+    if shares == 2:
+
+        @pl.when(me == 2)
+        def _():
+            tell(both_sem, me, other_vol)
+            pl.semaphore_wait(both_sem, 1)
+
+            @pl.loop(1, n)
+            def _(step):
+                tell(pass_sem, peer(step))
+
     @pl.when(me >= 2)
     def _():
-        pl.semaphore_wait(late_sem, 1)
         for dst in range(2):
             for m in range(parts):
                 copy_to(m, dst).start()
 
-    @pl.when(me >= n - 2)
-    def _():
-        main_copy(n - 1 - me).start()
-
-    main_copy(n - 1 - me).wait_recv()
+    if shares == 2:
+
+        @pl.when(me != 2)
+        def _():
+            pl.semaphore_wait(pass_sem, 1)
+
+    def hand_on(at):
+        main_copy(at).wait_recv()
+        if shares == 2:
+            pass_copy(at).start()
+
+    each_tile(hand_on)
+    for i in (7, 8):
+        fetch(i).wait()
+
+    def forward_group(m, group):
+        whole(m).wait_recv()
+        for at, d in enumerate(group):
+            re, im = x_forward(recvs[m][:, 2 * at, :], recvs[m][:, 2 * at + 1, :])
+            spec[0, d] = re
+            spec[1, d] = im
+
+    forward_group(0, HEAD_GROUPS[0])
+    if shares == 2:
+        each_tile(lambda at: pass_copy(at).wait_recv(), mine=False)
     slot_zero = lane_iota % half == 0
     for at in range(2 * slices):
         resp[at] = own_half[at] + main_recv[at]
@@ -347,21 +422,15 @@
             resp[at] = jnp.where(slot_zero, 0.5 * (here + edge), here)
             resp_mix[at] = jnp.where(slot_zero, 0.5 * (here - edge), 0.0)
 
-    for i in (7, 8):
-        fetch(i).wait()
-    for m, group in enumerate(GROUPS):
-        whole(m).wait_recv()
-        for at, d in enumerate(group):
-            re, im = x_forward(recvs[m][:, 2 * at, :], recvs[m][:, 2 * at + 1, :])
-            spec[0, d] = re
-            spec[1, d] = im
+    for m, group in enumerate(HEAD_GROUPS[1:], start=1):
+        forward_group(m, group)
 
     @pl.when(me == middle)
     def _():
         re, im = x_forward_conj(
             [
                 (recvs[m][:, 2 * at, :], recvs[m][:, 2 * at + 1, :])
-                for m, group in enumerate(GROUPS)
+                for m, group in enumerate(HEAD_GROUPS)
                 for at, _ in enumerate(group)
             ]
         )
@@ -414,7 +483,7 @@
         spec_mix[0] = re
         spec_mix[1] = im
 
-    for m, group in enumerate(GROUPS, start=parts + 2):
+    for m, group in enumerate(TAIL_GROUPS, start=parts + 2):
         for at, d in enumerate(group):
             re, im = spec[0, 0], spec[1, 0]
             rr, ri = resp[d], resp[slices + d]
@@ -430,7 +499,7 @@
 
             x_inverse(total[0], total[1], m, at)
         start(m)
-    for m, group in enumerate(GROUPS, start=parts + 2):
+    for m, group in enumerate(TAIL_GROUPS, start=parts + 2):
         whole(m).wait_recv()
         for at, d in enumerate(group):
             correction = y_inverse(m, at)
@@ -439,7 +508,9 @@
                 out_ref[d, :, cols] = vol_ref[d, :, cols] * correction[a * q : (a + 1) * q]
     for m in range(messages):
         whole(m).wait_send()
-    main_copy(n - 1 - me).wait_send()
+    each_tile(lambda at: main_copy(at).wait_send())
+    if shares == 2:
+        each_tile(lambda at: pass_copy(at).wait_send())
 
     @pl.when(me < middle)
     def _():
@@ -449,16 +520,17 @@
 def shards(volume, psf_spectra, background, measured):
     n = lax.axis_size("row")
     slices, q, length = volume.shape
+    shares = 2 if lax.axis_size("vol") % 2 == 0 else 1
     consts = tables(n, q)
     args = (volume, psf_spectra, background, measured, *consts)
-    grouped = [2 * len(group) for group in GROUPS]
-    counts = grouped + [2, 2] + grouped
+    sizes = lambda groups: [2 * len(group) for group in groups]
+    counts = sizes(HEAD_GROUPS) + [2, 2] + sizes(TAIL_GROUPS)
     in_vmem = pl.BlockSpec(memory_space=pltpu.VMEM)
     in_hbm = pl.BlockSpec(memory_space=pltpu.HBM)
     exchanged = [pltpu.VMEM((n, count, n), F32) for count in counts]
     tile = lambda *lead: pltpu.VMEM((*lead, n, n), F32)
     return pl.pallas_call(
-        functools.partial(kernel, n, q, slices, counts),
+        functools.partial(kernel, n, q, slices, counts, shares),
         out_shape=(
             jax.ShapeDtypeStruct(volume.shape, F32),
             jax.ShapeDtypeStruct(measured.shape, F32),
@@ -483,8 +555,11 @@
             pltpu.SemaphoreType.DMA((len(args),)),
             pltpu.SemaphoreType.DMA((len(counts),)),
             pltpu.SemaphoreType.DMA((len(counts),)),
+            pltpu.SemaphoreType.DMA((2, 2 * slices)),
+            pltpu.SemaphoreType.DMA((2, 2 * slices)),
             pltpu.SemaphoreType.DMA((2,)),
-            pltpu.SemaphoreType.DMA((2,)),
+            pltpu.SemaphoreType.REGULAR,
+            pltpu.SemaphoreType.REGULAR,
             pltpu.SemaphoreType.REGULAR,
         ],
         compiler_params=pltpu.CompilerParams(

time: 95.8 us -> 90.9 us (0.949)
  Pallas kernels: 92.6 us -> 87.7 us
    pallas_call x1, Pallas kernels: 92.6 us -> 87.7 us  [shards(): pl.pallas_call(functools.partial(kernel, n, q, slices, counts, shares), o...]
where the time goes in v2:
time: 90.9 us; the launch traced here: 90.8 us
  Pallas kernels  87.7 us (96%)
  local copies, waits for them, and re-layouts  2.46 us (3%)
    pallas_call x1, Pallas kernels, shards(): pl.pallas_call(functools.partial(kernel, n, q, slices, counts, shares), o...  87.7 us
    unnamed x4, local copies, waits for them, and re-layouts  2.46 us

profile of v2, /device:TPU:513, one launch (start us, length us, event | category | flops | bytes accessed | tf_op | source)
XLA Modules:
  0.0 90.8 jit_solution(16334838132871026549)
XLA Ops:
  0.6 87.7 %shard_map.122 = (f32[3,16,2048]{2,1,0:T(8,128)}, f32[16,2048]{1,0:T(8,128)}) custom-call(f32[3,16,2048]{2,1,0:T(8,128)} %refs_0_.1, bf16[2,3,16,2048]{3,2,1,0:T(8,128)(2,1)} %refs_1_.1, f32[16,2048]{1,0:T(8,128)} %refs_2_.1, f32[16,2048]{1,0:T(8,128)} %refs_3_.1, bf16[2,288,256]{2,1,0:T(8,128)(2,1)} %constant.14.clone.refs_4_, ...), custom_call_target="tpu_custom_call" | custom-call | tf_op jit(solution)/shard_map/pallas_call | solution.py:532
  88.3 0.0 copy-start
  88.3 1.8 %copy.15 = f32[3,16,2048]{2,1,0:T(8,128)} copy(f32[3,16,2048]{2,1,0:T(8,128)} %get-tuple-element.4) | data formatting | bytes 786432
  90.1 0.0 copy-done
  90.1 0.7 copy.16
Async XLA Ops:
  88.3 1.8 %copy-start = (f32[16,2048]{1,0:T(8,128)S(1)}, f32[16,2048]{1,0:T(8,128)}, u32[]{:S(2)}) copy-start(f32[16,2048]{1,0:T(8,128)} %get-tuple-element.5) | copy-start | bytes 393220

commit v3 on v2

--- a/solution.py
+++ b/solution.py
@@ -15,7 +15,7 @@
 NN = (((1,), (0,)), ((), ()))
 NT = (((1,), (1,)), ((), ()))
 HEAD_GROUPS = ((0, 1, 2),)
-TAIL_GROUPS = ((0, 1), (2,))
+TAIL_GROUPS = ((0,), (1, 2))
 
 
 def split_np(table):
@@ -126,7 +126,7 @@
 
     @pl.when(me >= 2)
     def _():
-        @pl.loop(1, n)
+        @pl.loop(1, n, unroll=8)
         def _(step):
             tell(barrier, peer(step))
 
@@ -311,7 +311,7 @@
 
     @pl.when(me == 1)
     def _():
-        @pl.loop(2, n)
+        @pl.loop(2, n, unroll=6)
         def _(dst):
             tell(late_sem, dst)
 
@@ -365,7 +365,7 @@
             tell(both_sem, me, other_vol)
             pl.semaphore_wait(both_sem, 1)
 
-            @pl.loop(1, n)
+            @pl.loop(1, n, unroll=8)
             def _(step):
                 tell(pass_sem, peer(step))
 
@@ -517,6 +517,19 @@
         row_copy(middle).wait_send()
 
 
+def place(*refs):
+    sources, targets, held, sems = refs[:2], refs[2:4], refs[4:6], refs[6]
+    reads = [pltpu.make_async_copy(sources[i], held[i], sems.at[0, i]) for i in range(2)]
+    writes = [pltpu.make_async_copy(held[i], targets[i], sems.at[1, i]) for i in range(2)]
+    for copy in reads:
+        copy.start()
+    for read, write in zip(reads, writes):
+        read.wait()
+        write.start()
+    for write in writes:
+        write.wait()
+
+
 def shards(volume, psf_spectra, background, measured):
     n = lax.axis_size("row")
     slices, q, length = volume.shape
@@ -529,12 +542,13 @@
     in_hbm = pl.BlockSpec(memory_space=pltpu.HBM)
     exchanged = [pltpu.VMEM((n, count, n), F32) for count in counts]
     tile = lambda *lead: pltpu.VMEM((*lead, n, n), F32)
-    return pl.pallas_call(
+    shapes = (
+        jax.ShapeDtypeStruct(volume.shape, F32),
+        jax.ShapeDtypeStruct(measured.shape, F32),
+    )
+    results = pl.pallas_call(
         functools.partial(kernel, n, q, slices, counts, shares),
-        out_shape=(
-            jax.ShapeDtypeStruct(volume.shape, F32),
-            jax.ShapeDtypeStruct(measured.shape, F32),
-        ),
+        out_shape=shapes,
         in_specs=[in_hbm] * len(args),
         out_specs=(in_vmem, in_vmem),
         scratch_shapes=[pltpu.VMEM(arg.shape, arg.dtype) for arg in args]
@@ -566,6 +580,15 @@
             collective_id=0, has_side_effects=True, vmem_limit_bytes=60 * 1024 * 1024
         ),
     )(*args)
+    return pl.pallas_call(
+        place,
+        out_shape=shapes,
+        in_specs=[in_hbm] * 2,
+        out_specs=(in_hbm, in_hbm),
+        scratch_shapes=[pltpu.VMEM(shape.shape, F32) for shape in shapes]
+        + [pltpu.SemaphoreType.DMA((2, 2))],
+        compiler_params=pltpu.CompilerParams(vmem_limit_bytes=60 * 1024 * 1024),
+    )(*results)
 
 
 def solution(mesh):

time: 90.9 us -> 89.9 us (0.989)
  local copies, waits for them, and re-layouts: 2.46 us -> 0 us
  Pallas kernels: 87.7 us -> 89.1 us
    unnamed x4 -> x0, local copies, waits for them, and re-layouts: 2.46 us -> none
    pallas_call x0 -> x1, Pallas kernels: none -> 1.81 us  [shards(): pl.pallas_call(place, out_shape=shapes, in_specs=[in_hbm] * 2, out_specs=...]
where the time goes in v3:
time: 89.9 us; the launch traced here: 89.8 us
  Pallas kernels  89.1 us (99%)
    pallas_call x1, Pallas kernels, shards(): pl.pallas_call(functools.partial(kernel, n, q, slices, counts, shares), o...  87.3 us
    pallas_call x1, Pallas kernels, shards(): pl.pallas_call(place, out_shape=shapes, in_specs=[in_hbm] * 2, out_specs=...  1.81 us

profile of v3, /device:TPU:513, one launch (start us, length us, event | category | flops | bytes accessed | tf_op | source)
XLA Modules:
  0.0 89.8 jit_solution(6690572915754494878)
XLA Ops:
  0.6 87.3 %shard_map.122 = (f32[3,16,2048]{2,1,0:T(8,128)}, f32[16,2048]{1,0:T(8,128)}) custom-call(f32[3,16,2048]{2,1,0:T(8,128)} %refs_0_.1, bf16[2,3,16,2048]{3,2,1,0:T(8,128)(2,1)} %refs_1_.1, f32[16,2048]{1,0:T(8,128)} %refs_2_.1, f32[16,2048]{1,0:T(8,128)} %refs_3_.1, bf16[2,288,256]{2,1,0:T(8,128)(2,1)} %constant.14.clone.refs_4_, ...), custom_call_target="tpu_custom_call" | custom-call | tf_op jit(solution)/shard_map/pallas_call | solution.py:549
  87.9 1.8 %shard_map.123 = (f32[3,16,2048]{2,1,0:T(8,128)}, f32[16,2048]{1,0:T(8,128)}) custom-call(f32[3,16,2048]{2,1,0:T(8,128)} %get-tuple-element.4.refs_0_, f32[16,2048]{1,0:T(8,128)} %get-tuple-element.5.refs_1_), custom_call_target="tpu_custom_call" | custom-call | tf_op jit(solution)/shard_map/pallas_call | solution.py:583

commit v4 on v3

--- a/solution.py
+++ b/solution.py
@@ -217,7 +217,7 @@
         out = dot3(split(turned), table(xmix_ref), NN)
         return out[:, :n], out[:, n:]
 
-    def x_forward_conj(fields):
+    def conjugates(fields):
         re_sum = im_sum = jnp.zeros((n, n), F32)
         for d, (re, im) in enumerate(fields):
             mine = (lane_iota >= d * q) & (lane_iota < (d + 1) * q)
@@ -225,7 +225,39 @@
                 re, im = pltpu.roll(re, d * q, 1), pltpu.roll(im, d * q, 1)
             re_sum = jnp.where(mine, re, re_sum)
             im_sum = jnp.where(mine, -im, im_sum)
-        return x_forward(re_sum, im_sum)
+        return re_sum, im_sum
+
+    def x_forward_both(re, im, fields):
+        re_conj, im_conj = conjugates(fields)
+        fields = jnp.concatenate(
+            [jnp.concatenate([re, re_conj], axis=1), jnp.concatenate([im, im_conj], axis=1)], axis=0
+        )
+        got = dot3(table(big_ref), split(fields), NN)
+        wr, wi = xtw_ref[0], xtw_ref[1]
+        turned = []
+        for at in range(2):
+            re, im = got[:n, at * n : (at + 1) * n], got[n:, at * n : (at + 1) * n]
+            turned.append(jnp.concatenate([re * wr - im * wi, re * wi + im * wr], axis=1))
+        out = dot3(split(jnp.concatenate(turned, axis=0)), table(xmix_ref), NN)
+        return (out[:n, :n], out[:n, n:]), (out[n:, :n], out[n:, n:])
+
+    def spectrum(d, m, at, sources):
+        def field(m, at):
+            return recvs[m][:, 2 * at, :], recvs[m][:, 2 * at + 1, :]
+
+        if not sources:
+            spec[0, d], spec[1, d] = x_forward(*field(m, at))
+            return
+
+        @pl.when(me != middle)
+        def _():
+            spec[0, d], spec[1, d] = x_forward(*field(m, at))
+
+        @pl.when(me == middle)
+        def _():
+            plain, conj = x_forward_both(*field(m, at), [field(*source) for source in sources])
+            spec[0, d], spec[1, d] = plain
+            spec_mix[0], spec_mix[1] = conj
 
     def x_inverse(re, im, m, at):
         mixed = dot3(split(jnp.concatenate([re, im], axis=1)), table(xmix_ref), NT)
@@ -390,12 +422,13 @@
     for i in (7, 8):
         fetch(i).wait()
 
+    heads = [(m, at) for m, group in enumerate(HEAD_GROUPS) for at in range(len(group))]
+
     def forward_group(m, group):
         whole(m).wait_recv()
+        last = m == parts - 1
         for at, d in enumerate(group):
-            re, im = x_forward(recvs[m][:, 2 * at, :], recvs[m][:, 2 * at + 1, :])
-            spec[0, d] = re
-            spec[1, d] = im
+            spectrum(d, m, at, heads if last and at == 0 else ())
 
     forward_group(0, HEAD_GROUPS[0])
     if shares == 2:
@@ -424,18 +457,6 @@
 
     for m, group in enumerate(HEAD_GROUPS[1:], start=1):
         forward_group(m, group)
-
-    @pl.when(me == middle)
-    def _():
-        re, im = x_forward_conj(
-            [
-                (recvs[m][:, 2 * at, :], recvs[m][:, 2 * at + 1, :])
-                for m, group in enumerate(HEAD_GROUPS)
-                for at, _ in enumerate(group)
-            ]
-        )
-        spec_mix[0] = re
-        spec_mix[1] = im
 
     sum_re = sum_im = jnp.zeros((n, n), F32)
     for d in range(slices):
@@ -473,15 +494,7 @@
     y_forward(jnp.concatenate(quotient, axis=0), parts + 1, 0)
     start(parts + 1)
     whole(parts + 1).wait_recv()
-    re, im = x_forward(recvs[parts + 1][:, 0, :], recvs[parts + 1][:, 1, :])
-    spec[0, 0] = re
-    spec[1, 0] = im
-
-    @pl.when(me == middle)
-    def _():
-        re, im = x_forward_conj([(recvs[parts + 1][:, 0, :], recvs[parts + 1][:, 1, :])])
-        spec_mix[0] = re
-        spec_mix[1] = im
+    spectrum(0, parts + 1, 0, [(parts + 1, 0)])
 
     for m, group in enumerate(TAIL_GROUPS, start=parts + 2):
         for at, d in enumerate(group):

time: 89.9 us -> 89.7 us (level)
  no operation moved by 1% of the time
where the time goes in v4:
time: 89.7 us; the launch traced here: 89.5 us
  Pallas kernels  88.9 us (99%)
    pallas_call x1, Pallas kernels, shards(): pl.pallas_call(functools.partial(kernel, n, q, slices, counts, shares), o...  87.1 us
    pallas_call x1, Pallas kernels, shards(): pl.pallas_call(place, out_shape=shapes, in_specs=[in_hbm] * 2, out_specs=...  1.81 us

profile of v4, /device:TPU:513, one launch (start us, length us, event | category | flops | bytes accessed | tf_op | source)
XLA Modules:
  0.0 89.5 jit_solution(347791630046787393)
XLA Ops:
  0.6 87.1 %shard_map.122 = (f32[3,16,2048]{2,1,0:T(8,128)}, f32[16,2048]{1,0:T(8,128)}) custom-call(f32[3,16,2048]{2,1,0:T(8,128)} %refs_0_.1, bf16[2,3,16,2048]{3,2,1,0:T(8,128)(2,1)} %refs_1_.1, f32[16,2048]{1,0:T(8,128)} %refs_2_.1, f32[16,2048]{1,0:T(8,128)} %refs_3_.1, bf16[2,288,256]{2,1,0:T(8,128)(2,1)} %constant.14.clone.refs_4_, ...), custom_call_target="tpu_custom_call" | custom-call | tf_op jit(solution)/shard_map/pallas_call | solution.py:562
  87.7 1.8 %shard_map.123 = (f32[3,16,2048]{2,1,0:T(8,128)}, f32[16,2048]{1,0:T(8,128)}) custom-call(f32[3,16,2048]{2,1,0:T(8,128)} %get-tuple-element.4.refs_0_, f32[16,2048]{1,0:T(8,128)} %get-tuple-element.5.refs_1_), custom_call_target="tpu_custom_call" | custom-call | tf_op jit(solution)/shard_map/pallas_call | solution.py:596
